TPU v7x, 32 devices: a whole 2x2x4 slice. The times are simulated.
32 devices in a mesh: dp: 8 (over y, x, core), seq: 4 (over z).
Axes of the slice: x: 2, y: 2, z: 4, core: 2. Of those that a mesh axis runs over, the one named last changes fastest.
Arguments:
- layer_input: bfloat16 [8, 512, 2048], P('dp', 'seq'), may hold values from -6 to 6
- cotangent: bfloat16 [8, 512, 2048], P('dp', 'seq'), may hold values from -6 to 6
- ln1_gain: float32 [2048], P('dp'), may hold values from 0.5 to 1.5
- ln1_bias: float32 [2048], P('dp'), may hold values from -3 to 3
- w_qkv: bfloat16 [2048, 6144], P('dp'), may hold values from -0.125 to 0.125
- b_qkv: float32 [6144], P('dp'), may hold values from -3 to 3
- w_out: bfloat16 [2048, 2048], P('dp'), may hold values from -0.5 to 0.5
- b_out: float32 [2048], P('dp'), may hold values from -3 to 3
- ln2_gain: float32 [2048], P('dp'), may hold values from 0.5 to 1.5
- ln2_bias: float32 [2048], P('dp'), may hold values from -3 to 3
- w_up: bfloat16 [2048, 8192], P('dp'), may hold values from -0.125 to 0.125
- b_up: float32 [8192], P('dp'), may hold values from -3 to 3
- w_down: bfloat16 [8192, 2048], P('dp'), may hold values from -0.0625 to 0.0625
- b_down: float32 [2048], P('dp'), may hold values from -3 to 3
Outputs:
- output: float32 [8, 512, 2048], P('dp', 'seq')
- input_grad: float32 [8, 512, 2048], P('dp', 'seq')
- ln1_gain_grad: float32 [2048], P('dp')
- ln1_bias_grad: float32 [2048], P('dp')
- w_qkv_grad: float32 [2048, 6144], P('dp')
- b_qkv_grad: float32 [6144], P('dp')
- w_out_grad: float32 [2048, 2048], P('dp')
- b_out_grad: float32 [2048], P('dp')
- ln2_gain_grad: float32 [2048], P('dp')
- ln2_bias_grad: float32 [2048], P('dp')
- w_up_grad: float32 [2048, 8192], P('dp')
- b_up_grad: float32 [8192], P('dp')
- w_down_grad: float32 [8192, 2048], P('dp')
- b_down_grad: float32 [2048], P('dp')
All inputs are finite; a program needn't handle non-finite values.
Results may differ from a plain program's by a relative error of at most 0.029.
Values may be sent and summed in bfloat16 or wider, within the bound.
A program may use at most 640 MiB of HBM per device.

v0:
```python
import jax
import jax.numpy as jnp
from jax import lax
from jax.sharding import PartitionSpec as P

H = 8
HD = 256
ROT = 64
epsilon = 1e-05
masked_fill = -1e30


def dot(a, b, contract):
    return lax.dot_general(a, b, (contract, ((), ())), preferred_element_type=jnp.float32)


def normalize(rows):
    center = rows - jnp.mean(rows, axis=-1, keepdims=True)
    factor = lax.rsqrt(jnp.mean(center * center, axis=-1, keepdims=True) + epsilon)
    return (center * factor, factor)


def angles(positions):
    half = ROT // 2
    freqs = 10000.0 ** (-2.0 * jnp.arange(half).astype(positions.dtype) / ROT)
    theta = positions[:, None] * freqs[None, :]
    return (jnp.cos(theta), jnp.sin(theta))


def rotate(tensor, cosine, sine, direction):
    half = ROT // 2
    first_half = tensor[..., :half]
    second_half = tensor[..., half:ROT]
    return jnp.concatenate(
        [
            first_half * cosine - direction * second_half * sine,
            second_half * cosine + direction * first_half * sine,
            tensor[..., ROT:],
        ],
        axis=-1,
    )


def gather_dp(rows):
    return lax.all_gather(rows, "dp", axis=0, tiled=True)


def gather_seq(shard):
    return lax.all_gather(shard, "seq", axis=0, tiled=False)


def scatter_dp(rows):
    return lax.psum_scatter(rows, "dp", scatter_dimension=0, tiled=True)


def exchange_sum(partial, n_seq):
    slabs = partial.astype(jnp.bfloat16).reshape(n_seq, partial.shape[0] // n_seq, partial.shape[1])
    got = lax.all_to_all(slabs, "seq", split_axis=0, concat_axis=0, tiled=True)
    return jnp.sum(got.astype(jnp.float32), axis=0)


def make_local(n_dp, n_seq):

    def local(
        layer_input,
        cotangent,
        ln1_gain,
        ln1_bias,
        w_qkv,
        b_qkv,
        w_out,
        b_out,
        ln2_gain,
        ln2_bias,
        w_up,
        b_up,
        w_down,
        b_down,
    ):
        f32, bf16 = (jnp.float32, jnp.bfloat16)
        _, tok_local, width = layer_input.shape
        length = tok_local * n_seq
        own = width // n_dp
        ff = w_up.shape[1]
        ff_own = ff // n_dp
        unit = ff_own // n_seq
        heads = H // n_seq
        z = lax.axis_index("seq")
        up_own = lax.dynamic_index_in_dim(
            w_up.reshape(own, n_dp, n_seq, unit), z, 2, keepdims=False
        ).reshape(own, n_dp * unit)
        up_w = gather_dp(up_own)
        down_own = lax.dynamic_slice_in_dim(w_down, z * unit, unit, 0)
        down_w = gather_dp(down_own)
        qkv_own = lax.dynamic_slice_in_dim(
            w_qkv.reshape(own, 3, H, HD), z * heads, heads, 2
        ).reshape(own, 3 * heads * HD)
        triple_w = gather_dp(qkv_own)
        owners = n_dp // n_seq
        piece = own // n_dp
        spread = lax.all_to_all(
            w_out.reshape(n_dp, piece, width), "dp", split_axis=0, concat_axis=0, tiled=True
        )
        out_own = lax.dynamic_slice_in_dim(spread, z * owners, owners, 0)
        out_w = (
            lax.all_gather(out_own, "dp", axis=0, tiled=False)
            .transpose(1, 0, 2, 3)
            .reshape(owners * own, width)
        )
        packed = jnp.concatenate(
            [ln1_gain, ln1_bias, ln2_gain, ln2_bias, b_out, b_down, b_qkv, b_up]
        )
        gathered = lax.all_gather(packed, "dp", axis=0, tiled=False)
        gain_one, shift_one, gain_two, shift_two, out_b, down_b = (
            gathered[:, k * own : (k + 1) * own].reshape(width) for k in range(6)
        )
        base = 6 * own
        triple_b = lax.dynamic_slice_in_dim(
            gathered[:, base : base + 3 * own].reshape(3, H, HD), z * heads, heads, 1
        ).reshape(3 * heads * HD)
        up_b = lax.dynamic_index_in_dim(
            gathered[:, base + 3 * own :].reshape(n_dp, n_seq, unit), z, 1, keepdims=False
        ).reshape(n_dp * unit)
        tokens = gather_seq(layer_input.reshape(tok_local, width)).reshape(length, width)
        incoming = gather_seq(cotangent.reshape(tok_local, width)).reshape(length, width)
        normed, _ = normalize(tokens.astype(f32))
        mlp_in = (normed * gain_two + shift_two).astype(bf16)
        attn_in = (normed * gain_one + shift_one).astype(bf16)
        inner = dot(mlp_in, up_w, ((1,), (0,))) + up_b
        cumulative = 0.5 * (1.0 + lax.erf(inner * 0.7071067811865476))
        hidden = (inner * cumulative).astype(bf16)
        slope = cumulative + inner * jnp.exp(-0.5 * inner * inner) * 0.3989422804014327
        down_grad = dot(hidden, incoming, ((0,), (0,))).astype(bf16)
        inner_grad = dot(incoming, down_w, ((1,), (1,))) * slope
        inner_grad_b = inner_grad.astype(bf16)
        up_grad = dot(mlp_in, inner_grad_b, ((0,), (0,))).astype(bf16)
        mlp_out = dot(hidden, down_w, ((1,), (0,)))
        mlp_in_grad = dot(inner_grad_b, up_w, ((1,), (1,)))
        b_up_grad = jnp.sum(inner_grad, axis=0)
        ln2_gain_grad = jnp.sum(mlp_in_grad * normed, axis=0)
        ln2_bias_grad = jnp.sum(mlp_in_grad, axis=0)
        cosine, sine = angles(jnp.arange(length, dtype=jnp.int32).astype(f32))
        cosine, sine = (cosine[:, None, :], sine[:, None, :])
        triple = (dot(attn_in, triple_w, ((1,), (0,))) + triple_b).reshape(length, 3, heads, HD)
        queries = rotate(triple[:, 0], cosine, sine, 1.0).astype(bf16)
        key_rows = rotate(triple[:, 1], cosine, sine, 1.0).astype(bf16)
        values = triple[:, 2].astype(bf16)
        scores = jnp.einsum("qhd,khd->hqk", queries, key_rows, preferred_element_type=f32) * HD ** (
            -0.5
        )
        order = jnp.arange(length, dtype=jnp.int32)
        scores = jnp.where((order[None, :] <= order[:, None])[None], scores, masked_fill)
        top = jnp.max(scores, axis=-1, keepdims=True)
        logsum = top + jnp.log(jnp.sum(jnp.exp(scores - top), axis=-1, keepdims=True))
        probs_f = jnp.exp(scores - logsum)
        probs = probs_f.astype(bf16)
        context = jnp.einsum("hqk,khd->qhd", probs, values, preferred_element_type=f32).astype(bf16)
        merged = context.reshape(length, heads * HD)
        attended = dot(merged, out_w, ((1,), (0,)))
        out_grad = dot(merged, incoming, ((0,), (0,))).astype(bf16)
        context_grad = dot(incoming, out_w, ((1,), (1,))).astype(bf16).reshape(length, heads, HD)
        delta = jnp.sum(context_grad.astype(f32) * context.astype(f32), axis=-1)
        value_grad = jnp.einsum(
            "hqk,qhd->khd", probs, context_grad, preferred_element_type=f32
        ).astype(bf16)
        prob_grad = jnp.einsum("qhd,khd->hqk", context_grad, values, preferred_element_type=f32)
        score_grad = (probs_f * (prob_grad - delta.T[:, :, None]) * HD ** (-0.5)).astype(bf16)
        query_grad = jnp.einsum(
            "hqk,khd->qhd", score_grad, key_rows, preferred_element_type=f32
        ).astype(bf16)
        key_grad = jnp.einsum(
            "hqk,qhd->khd", score_grad, queries, preferred_element_type=f32
        ).astype(bf16)
        triple_grad = jnp.stack(
            [
                rotate(query_grad.astype(f32), cosine, sine, -1.0),
                rotate(key_grad.astype(f32), cosine, sine, -1.0),
                value_grad.astype(f32),
            ],
            axis=1,
        ).reshape(length, 3 * heads * HD)
        triple_grad_b = triple_grad.astype(bf16)
        b_qkv_grad = jnp.sum(triple_grad, axis=0)
        qkv_grad = dot(attn_in, triple_grad_b, ((0,), (0,))).astype(bf16)
        attn_in_grad = dot(triple_grad_b, triple_w, ((1,), (1,)))
        ln1_gain_grad = jnp.sum(attn_in_grad * normed, axis=0)
        ln1_bias_grad = jnp.sum(attn_in_grad, axis=0)
        rows = layer_input.reshape(tok_local, width).astype(f32)
        grad_rows = cotangent.reshape(tok_local, width).astype(f32)
        output = rows + (out_b + down_b) + exchange_sum(attended + mlp_out, n_seq)
        scaled = exchange_sum(attn_in_grad * gain_one + mlp_in_grad * gain_two, n_seq)
        normed_own, factor_own = normalize(rows)
        input_grad = grad_rows + factor_own * (
            scaled
            - jnp.mean(scaled, axis=-1, keepdims=True)
            - normed_own * jnp.mean(scaled * normed_own, axis=-1, keepdims=True)
        )
        down_part = gather_seq(scatter_dp(down_grad))
        down_full = down_part.reshape(ff_own, width).astype(f32)
        up_part = gather_seq(scatter_dp(up_grad))
        up_full = (
            up_part.reshape(n_seq, own, n_dp, unit)
            .transpose(1, 2, 0, 3)
            .reshape(own, ff)
            .astype(f32)
        )
        out_part = gather_seq(
            scatter_dp(
                out_grad.reshape(owners, n_dp, piece, width)
                .transpose(1, 0, 2, 3)
                .reshape(n_dp * owners * piece, width)
            )
        )
        out_full = (
            lax.all_to_all(
                out_part.reshape(n_dp, piece, width), "dp", split_axis=0, concat_axis=0, tiled=True
            )
            .reshape(own, width)
            .astype(f32)
        )
        qkv_part = gather_seq(scatter_dp(qkv_grad))
        qkv_full = (
            qkv_part.reshape(n_seq, own, 3, heads * HD)
            .transpose(1, 2, 0, 3)
            .reshape(own, 3 * width)
            .astype(f32)
        )
        here = jnp.arange(n_seq) == z
        b_up_wide = jnp.where(here[None, :, None], b_up_grad.reshape(n_dp, 1, unit), 0.0).reshape(
            n_dp, ff_own
        )
        b_qkv_wide = jnp.where(
            here[None, :, None], b_qkv_grad.reshape(3, 1, heads * HD), 0.0
        ).reshape(n_dp, 3 * own)
        b_down_grad = jnp.sum(grad_rows, axis=0)
        small = jnp.concatenate(
            [
                ln1_gain_grad.reshape(n_dp, own),
                ln1_bias_grad.reshape(n_dp, own),
                ln2_gain_grad.reshape(n_dp, own),
                ln2_bias_grad.reshape(n_dp, own),
                b_down_grad.reshape(n_dp, own),
                b_qkv_wide,
                b_up_wide,
            ],
            axis=1,
        )
        small = lax.psum(small, ("dp", "seq"))
        mine = lax.dynamic_index_in_dim(small, lax.axis_index("dp"), 0, keepdims=False)
        g1, s1, g2, s2, bd = (mine[k * own : (k + 1) * own] for k in range(5))
        bq = mine[5 * own : 8 * own]
        bu = mine[8 * own :]
        return (
            output.reshape(layer_input.shape),
            input_grad.reshape(layer_input.shape),
            g1,
            s1,
            qkv_full,
            bq,
            out_full,
            bd,
            g2,
            s2,
            up_full,
            bu,
            down_full,
            bd,
        )

    return local


def solution(mesh):
    vector, matrix, tokens = (P("dp"), P("dp", None), P("dp", "seq", None))
    in_specs = (
        tokens,
        tokens,
        vector,
        vector,
        matrix,
        vector,
        matrix,
        vector,
        vector,
        vector,
        matrix,
        vector,
        matrix,
        vector,
    )
    out_specs = (
        tokens,
        tokens,
        vector,
        vector,
        matrix,
        vector,
        matrix,
        vector,
        vector,
        vector,
        matrix,
        vector,
        matrix,
        vector,
    )
    local = make_local(mesh.shape["dp"], mesh.shape["seq"])
    return jax.shard_map(local, mesh=mesh, in_specs=in_specs, out_specs=out_specs, check_vma=False)
```

profile of v0, /device:TPU:0, one launch (start us, length us, event | category | flops | bytes accessed | tf_op | source)
XLA Modules:
  0.0 955.7 jit_solution(7400377994347457688)
XLA Ops:
  7.9 5.3 all-to-all-start
  13.3 15.4 %all-to-all-done = bf16[8,32,2048]{2,1,0:T(8,128)(2,1)} async-done(((bf16[8,32,2048]{2,1,0:T(8,128)(2,1)}), bf16[8,32,2048]{2,1,0:T(8,128)(2,1)}, u32[]{:S(2)}, u32[]{:S(2)}) %all-to-all-start) | async-done | bytes 1048608 | tf_op jit(solution)/shard_map/all_to_all | solution.py:101
  34.5 6.4 copy.92
  41.0 2.3 constant_dynamic-slice_fusion.2
  43.4 2.3 constant_dynamic-slice_fusion.1
  46.0 8.5 all-gather.6
  61.5 3.4 add_convert_fusion.4
  64.9 21.6 %all-gather.28.cloned.1.call-done = bf16[16,32,2048]{2,1,0:T(8,128)(2,1)} async-done(((bf16[2,32,2048]{2,1,0:T(8,128)(2,1)}), bf16[16,32,2048]{2,1,0:T(8,128)(2,1)}) %all-gather.28.cloned.1.call-update) | async-done | bytes 2097168 | tf_op jit(solution)/shard_map/all_gather | solution.py:106
  88.2 45.5 %all-gather.26.cloned.1.call-done = bf16[4,128,2048]{2,1,0:T(8,128)(2,1)} async-done(((bf16[1,128,2048]{2,1,0:T(8,128)(2,1)}), bf16[4,128,2048]{2,1,0:T(8,128)(2,1)}) %all-gather.26.cloned.1.call-update) | async-done | bytes 2097168 | tf_op jit(solution)/shard_map/all_gather | solution.py:49
  133.7 3.7 convolution_convert_fusion.4
  137.4 42.8 %all-gather.20.cloned.1.call-done = bf16[2048,1536]{1,0:T(8,128)(2,1)} async-done(((bf16[256,1536]{1,0:T(8,128)(2,1)}), bf16[2048,1536]{1,0:T(8,128)(2,1)}) %all-gather.20.cloned.1.call-update) | async-done | bytes 6291472 | tf_op jit(solution)/shard_map/all_gather | solution.py:45
  180.3 8.5 convolution_add_fusion
  188.8 3.9 reshape.392
  205.0 3.8 add_convert_fusion
  218.8 8.2 convolution_convert_fusion.2
  227.1 11.4 %all-gather.22.cloned.1.call-done = bf16[2048,2048]{0,1:T(8,128)(2,1)} async-done(((bf16[256,2048]{0,1:T(8,128)(2,1)}), bf16[2048,2048]{0,1:T(8,128)(2,1)}) %all-gather.22.cloned.1.call-update) | async-done | bytes 8388624 | tf_op jit(solution)/shard_map/all_gather | solution.py:45
  238.5 8.9 multiply_convert_fusion
  247.4 47.7 %all-gather.24.cloned.1.call-done = bf16[2048,2048]{1,0:T(8,128)(2,1)} async-done(((bf16[256,2048]{1,0:T(8,128)(2,1)}), bf16[2048,2048]{1,0:T(8,128)(2,1)}) %all-gather.24.cloned.1.call-update) | async-done | bytes 8388624 | tf_op jit(solution)/shard_map/all_gather | solution.py:45
  295.1 10.7 %fusion.43 = (f32[2048]{0:T(1024)S(1)}, bf16[512,2048]{1,0:T(8,128)(2,1)S(1)}) fusion(f32[512,2048]{1,0:T(8,128)} %get-tuple-element.92, f32[2048]{0:T(1024)S(1)} %bitcast.207, bf16[2048,2048]{1,0:T(8,128)(2,1)} %all-gather.24.cloned.1.call-done, bf16[512,2048]{1,0:T(8,128)(2,1)} %bitcast.216), kind=kOutput, calls=%fused_computation.142 | convolution fusion | flops 4307548160 | bytes 16793600 | tf_op jit(solution)/shard_map/dot_general | solution.py:14
  307.1 6.8 convolution_convert_fusion.1
  315.5 8.5 convolution_convert_fusion
  325.5 5.8 fusion.45
  331.3 10.5 %fusion.38 = (f32[2048]{0:T(1024)S(1)}, f32[2048]{0:T(1024)S(1)}, bf16[512,2048]{1,0:T(8,128)(2,1)}, f32[2048]{0:T(1024)S(1)}, f32[2048]{0:T(1024)S(1)}) fusion(f32[512]{0:T(512)S(1)} %copy-done.36, f32[512]{0:T(512)S(1)} %copy-done.34, bf16[4,128,2048]{2,1,0:T(8,128)(2,1)S(1)} %copy-done.1, f32[2048]{0:T(1024)S(1)} %bitcast.200, ...), kind=kOutput, calls=%fused_computation.137 | convolution fusion | flops 4308590592 | bytes 18927616 | tf_op jit(solution)/shard_map/dot_general | solution.py:14
  341.8 4.7 all-to-all-start.2
  346.5 7.1 fusion.44
  353.6 2.6 add_convert_fusion.2
  356.2 39.2 %all-to-all-done.2 = bf16[4,128,2048]{2,1,0:T(8,128)(2,1)} async-done(((bf16[4,128,2048]{2,1,0:T(8,128)(2,1)}), bf16[4,128,2048]{2,1,0:T(8,128)(2,1)}, u32[]{:S(2)}, u32[]{:S(2)}) %all-to-all-start.2) | async-done | bytes 2097184 | tf_op jit(solution)/shard_map/all_to_all | solution.py:58
  395.4 4.5 all-to-all-start.1
  402.3 2.3 convert_reduce_fusion
  404.9 43.0 %all-to-all-done.1 = bf16[4,128,2048]{2,1,0:T(8,128)(2,1)} async-done(((bf16[4,128,2048]{2,1,0:T(8,128)(2,1)}), bf16[4,128,2048]{2,1,0:T(8,128)(2,1)}, u32[]{:S(2)}, u32[]{:S(2)}) %all-to-all-start.1) | async-done | bytes 2097184 | tf_op jit(solution)/shard_map/all_to_all | solution.py:58
  453.3 27.5 %reduce-scatter.9.cloned.1.call-done = bf16[256,2048]{1,0:T(8,128)(2,1)} async-done(((bf16[2048,2048]{1,0:T(8,128)(2,1)}), bf16[256,2048]{1,0:T(8,128)(2,1)}) %reduce-scatter.9.cloned.1.call-update) | async-done | bytes 1048592 | tf_op jit(solution)/shard_map/reduce_scatter | solution.py:53
  480.9 75.3 %reduce-scatter.11.cloned.1.call-done = bf16[256,2048]{1,0:T(8,128)(2,1)} async-done(((bf16[2048,2048]{1,0:T(8,128)(2,1)}), bf16[256,2048]{1,0:T(8,128)(2,1)}) %reduce-scatter.11.cloned.1.call-update) | async-done | bytes 1048592 | tf_op jit(solution)/shard_map/reduce_scatter | solution.py:53
  556.3 29.6 %all-gather.32.cloned.1.call-done = bf16[256,2048]{1,0:T(8,128)(2,1)} async-done(((bf16[64,2048]{1,0:T(8,128)(2,1)}), bf16[256,2048]{1,0:T(8,128)(2,1)}) %all-gather.32.cloned.1.call-update) | async-done | bytes 1048592 | tf_op jit(solution)/shard_map/all_gather | solution.py:49
  585.8 3.9 all-to-all-start.3
  589.7 15.5 %all-to-all-done.3 = bf16[8,32,2048]{2,1,0:T(8,128)(2,1)S(1)} async-done(((bf16[8,32,2048]{2,1,0:T(8,128)(2,1)}), bf16[8,32,2048]{2,1,0:T(8,128)(2,1)S(1)}, u32[]{:S(2)}, u32[]{:S(2)}) %all-to-all-start.3) | async-done | bytes 1048608 | tf_op jit(solution)/shard_map/all_to_all | solution.py:215
  606.9 107.3 %all-reduce.2.cloned.1.call-done = f32[8,3072]{1,0:T(8,128)} async-done(((f32[8,3072]{1,0:T(8,128)}), f32[8,3072]{1,0:T(8,128)}) %all-reduce.2.cloned.1.call-update) | async-done | bytes 98320 | tf_op jit(solution)/shard_map/psum | solution.py:248
  718.5 61.7 %all-gather.30.cloned.1.call-done = bf16[1024,1536]{1,0:T(8,128)(2,1)} async-done(((bf16[256,1536]{1,0:T(8,128)(2,1)}), bf16[1024,1536]{1,0:T(8,128)(2,1)}) %all-gather.30.cloned.1.call-update) | async-done | bytes 3145744 | tf_op jit(solution)/shard_map/all_gather | solution.py:49
  780.2 5.4 copy.105
  785.6 8.2 reshape.417
  793.8 6.6 copy.106
  800.4 6.6 copy.109
  806.9 54.1 %all-gather.34.cloned.1.call-done = bf16[1024,2048]{1,0:T(8,128)(2,1)} async-done(((bf16[256,2048]{1,0:T(8,128)(2,1)}), bf16[1024,2048]{1,0:T(8,128)(2,1)}) %all-gather.34.cloned.1.call-update) | async-done | bytes 4194320 | tf_op jit(solution)/shard_map/all_gather | solution.py:49
  861.0 4.3 copy.135
  865.3 4.1 bitcast_bitcast_fusion
  869.5 12.4 %copy.108 = f32[256,8,4,256]{3,2,1,0:T(4,128)} copy(f32[256,8,4,256]{3,1,0,2:T(8,128)} %bitcast_bitcast_fusion) | data formatting | bytes 16777216 | tf_op jit(solution)/shard_map/convert_element_type | solution.py:205
  881.9 10.7 %reshape.415 = f32[256,8192]{1,0:T(8,128)} reshape(f32[256,8,4,256]{3,2,1,0:T(4,128)} %copy.108) | data formatting | bytes 16777216 | tf_op jit(solution)/shard_map/convert_element_type | solution.py:205
  892.6 49.1 %all-gather.36.cloned.1.call-done = bf16[1024,2048]{1,0:T(8,128)(2,1)} async-done(((bf16[256,2048]{1,0:T(8,128)(2,1)}), bf16[1024,2048]{1,0:T(8,128)(2,1)}) %all-gather.36.cloned.1.call-update) | async-done | bytes 4194320 | tf_op jit(solution)/shard_map/all_gather | solution.py:49
  941.7 6.7 convert_element_type.310
  (231 shorter events, 56.2 us)
Async XLA Ops:
  7.2 24.1 %copy-start.12 = (bf16[256,6144]{1,0:T(8,128)(2,1)S(1)}, bf16[256,6144]{1,0:T(8,128)(2,1)}, u32[]{:S(2)}) copy-start(bf16[256,6144]{1,0:T(8,128)(2,1)} %param.18) | copy-start | bytes 9437188
  7.2 50.8 %all-gather.18.cloned.1.call-start = ((), (), s32[]{:S(2)}) async-start(), calls=%async_computation.8 | async-start | bytes 2621440 | tf_op jit(solution)/shard_map/all_gather | solution.py:49
  7.9 20.8 %all-to-all-start = ((bf16[8,32,2048]{2,1,0:T(8,128)(2,1)}), bf16[8,32,2048]{2,1,0:T(8,128)(2,1)}, u32[]{:S(2)}, u32[]{:S(2)}) async-start(bf16[8,32,2048]{2,1,0:T(8,128)(2,1)} %bitcast.187), calls=%async_computation | async-start | bytes 2097152 | tf_op jit(solution)/shard_map/all_to_all | solution.py:101
  13.3 73.2 %all-gather.28.cloned.1.call-start = ((), (), s32[]{:S(2)}) async-start(), calls=%async_computation.18 | async-start | bytes 2359296 | tf_op jit(solution)/shard_map/all_gather | solution.py:106
  30.4 103.3 %all-gather.26.cloned.1.call-start = ((), (), s32[]{:S(2)}) async-start(), calls=%async_computation.12 | async-start | bytes 2621440 | tf_op jit(solution)/shard_map/all_gather | solution.py:49
  31.2 149.1 %all-gather.20.cloned.1.call-start = ((), (), s32[]{:S(2)}) async-start(), calls=%async_computation.9 | async-start | bytes 7077888 | tf_op jit(solution)/shard_map/all_gather | solution.py:45
  34.5 204.0 %all-gather.22.cloned.1.call-start = ((), (), s32[]{:S(2)}) async-start(), calls=%async_computation.10 | async-start | bytes 9437184 | tf_op jit(solution)/shard_map/all_gather | solution.py:45
  40.9 4.9 copy-start.40
  40.9 4.9 copy-start.41
  40.9 4.9 copy-start.42
  40.9 4.9 copy-start.43
  40.9 4.9 copy-start.44
  40.9 5.0 copy-start.45
  40.9 5.0 copy-start.38
  40.9 5.0 copy-start.39
  43.3 251.8 %all-gather.24.cloned.1.call-start = ((), (), s32[]{:S(2)}) async-start(), calls=%async_computation.11 | async-start | bytes 9437184 | tf_op jit(solution)/shard_map/all_gather | solution.py:45
  45.7 356.4 %reduce-scatter.7.cloned.1.call-start = ((), (), s32[]{:S(2)}) async-start(), calls=%async_computation.15 | async-start | bytes 2359296 | tf_op jit(solution)/shard_map/reduce_scatter | solution.py:53
  58.0 2.2 copy-start
  60.1 4.8 copy-start.33
  61.5 3.4 copy-start.35
  88.2 49.2 %copy-start.6 = (bf16[2,8,32,2048]{3,2,1,0:T(8,128)(2,1)}, bf16[2,8,32,2048]{3,2,1,0:T(8,128)(2,1)S(1)}, u32[]{:S(2)}) copy-start(bf16[2,8,32,2048]{3,2,1,0:T(8,128)(2,1)S(1)} %copy.91) | copy-start | bytes 6291460
  194.6 2.2 copy-start.14
  200.6 1.6 copy-start.46
  205.0 247.6 %reduce-scatter.5.cloned.1.call-start = ((), (), s32[]{:S(2)}) async-start(), calls=%async_computation.14 | async-start | bytes 7077888 | tf_op jit(solution)/shard_map/reduce_scatter | solution.py:53
  205.0 3.8 copy-start.32
  227.0 11.5 %copy-start.19 = (bf16[512,2048]{1,0:T(8,128)(2,1)S(1)}, bf16[512,2048]{1,0:T(8,128)(2,1)}, u32[]{:S(2)}) copy-start(bf16[512,2048]{1,0:T(8,128)(2,1)} %get-tuple-element.54) | copy-start | bytes 6291460
  227.0 253.8 %reduce-scatter.9.cloned.1.call-start = ((), (), s32[]{:S(2)}) async-start(), calls=%async_computation.16 | async-start | bytes 9437184 | tf_op jit(solution)/shard_map/reduce_scatter | solution.py:53
  313.9 1.6 copy-start.47
  313.9 242.3 %reduce-scatter.11.cloned.1.call-start = ((), (), s32[]{:S(2)}) async-start(), calls=%async_computation.17 | async-start | bytes 9437184 | tf_op jit(solution)/shard_map/reduce_scatter | solution.py:53
  325.4 5.8 copy-start.1
  325.4 5.8 copy-start.34
  325.4 5.8 copy-start.36
  325.4 5.8 copy-start.50
  341.8 4.7 copy-start.48
  341.8 53.6 %all-to-all-start.2 = ((bf16[4,128,2048]{2,1,0:T(8,128)(2,1)}), bf16[4,128,2048]{2,1,0:T(8,128)(2,1)}, u32[]{:S(2)}, u32[]{:S(2)}) async-start(bf16[4,128,2048]{2,1,0:T(8,128)(2,1)} %bitcast.31), calls=%async_computation.2 | async-start | bytes 4194304 | tf_op jit(solution)/shard_map/all_to_all | solution.py:58
  346.5 7.1 copy-start.7
  346.5 7.1 copy-start.11
  356.2 43.8 %copy-start.2 = (bf16[1,128,2048]{2,1,0:T(8,128)(2,1)S(1)}, bf16[1,128,2048]{2,1,0:T(8,128)(2,1)}, u32[]{:S(2)}) copy-start(bf16[1,128,2048]{2,1,0:T(8,128)(2,1)} %param.14) | copy-start | bytes 1572868
  356.2 44.3 %copy-start.4 = (f32[512,1,2,256]{3,0,2,1:T(8,128)S(1)}, f32[512,1,2,256]{3,0,2,1:T(8,128)}, u32[]{:S(2)}) copy-start(f32[512,1,2,256]{3,0,2,1:T(8,128)} %copy-done.3) | copy-start | bytes 3145732
  395.4 52.4 %all-to-all-start.1 = ((bf16[4,128,2048]{2,1,0:T(8,128)(2,1)}), bf16[4,128,2048]{2,1,0:T(8,128)(2,1)}, u32[]{:S(2)}, u32[]{:S(2)}) async-start(bf16[4,128,2048]{2,1,0:T(8,128)(2,1)} %bitcast.15), calls=%async_computation.1 | async-start | bytes 4194304 | tf_op jit(solution)/shard_map/all_to_all | solution.py:58
  399.9 186.0 %all-gather.32.cloned.1.call-start = ((), (), s32[]{:S(2)}) async-start(), calls=%async_computation.20 | async-start | bytes 1310720 | tf_op jit(solution)/shard_map/all_gather | solution.py:49
  402.1 312.1 %all-reduce.2.cloned.1.call-start = ((), (), s32[]{:S(2)}) async-start(), calls=%async_computation.13 | async-start | bytes 196608 | tf_op jit(solution)/shard_map/psum | solution.py:248
  404.5 45.4 %copy-start.13 = (bf16[1,128,2048]{2,1,0:T(8,128)(2,1)S(1)}, bf16[1,128,2048]{2,1,0:T(8,128)(2,1)}, u32[]{:S(2)}) copy-start(bf16[1,128,2048]{2,1,0:T(8,128)(2,1)} %param.15) | copy-start | bytes 1572868
  452.5 327.7 %all-gather.30.cloned.1.call-start = ((), (), s32[]{:S(2)}) async-start(), calls=%async_computation.19 | async-start | bytes 3932160 | tf_op jit(solution)/shard_map/all_gather | solution.py:49
  453.3 407.8 %all-gather.34.cloned.1.call-start = ((), (), s32[]{:S(2)}) async-start(), calls=%async_computation.21 | async-start | bytes 5242880 | tf_op jit(solution)/shard_map/all_gather | solution.py:49
  480.9 460.8 %all-gather.36.cloned.1.call-start = ((), (), s32[]{:S(2)}) async-start(), calls=%async_computation.22 | async-start | bytes 5242880 | tf_op jit(solution)/shard_map/all_gather | solution.py:49
  585.8 19.4 %all-to-all-start.3 = ((bf16[8,32,2048]{2,1,0:T(8,128)(2,1)}), bf16[8,32,2048]{2,1,0:T(8,128)(2,1)S(1)}, u32[]{:S(2)}, u32[]{:S(2)}) async-start(bf16[8,32,2048]{2,1,0:T(8,128)(2,1)} %bitcast.188), calls=%async_computation.5 | async-start | bytes 2097152 | tf_op jit(solution)/shard_map/all_to_all | solution.py:215
  715.6 232.7 %copy-start.37 = (f32[1,256]{1,0:T(1,128)}, f32[1,256]{1,0:T(1,128)S(1)}, u32[]{:S(2)}) copy-start(f32[1,256]{1,0:T(1,128)S(1)} %get-tuple-element.77) | copy-start | bytes 3076
  (22 other events, 29.1 us)
Sparse Core Ops, SparseCore 0:
  9.6 48.3 all-gather.17
  59.9 26.5 all-gather.27
  88.1 45.6 all-gather.25
  136.1 44.1 all-gather.19
  182.6 55.8 all-gather.21
  240.8 54.2 all-gather.23
  298.4 41.1 reduce-scatter.6
  343.5 61.7 reduce-scatter.4
  409.3 71.4 reduce-scatter.8
  484.7 71.4 reduce-scatter.10
  557.8 27.9 all-gather.31
  591.3 122.9 all-reduce.1
  715.8 64.3 all-gather.29
  781.6 79.3 all-gather.33
  862.4 79.2 all-gather.35
where the time goes:
time: 961 us; the launch traced here: 956 us
  waiting for transfers between devices  690 us (72%)
  local copies, waits for them, and re-layouts  102 us (11%)
  matrix products  87.6 us (9%)
  other arithmetic  33.9 us (4%)
  starting transfers between devices  19 us (2%)
  between operations  15.1 us (2%)
    all_gather x6, waiting for transfers between devices, gather_seq(): return lax.all_gather(shard, 'seq', axis=0, tiled=False)  241 us
    psum x1, waiting for transfers between devices, local(): small = lax.psum(small, ('dp', 'seq'))  107 us
    reduce_scatter x4, waiting for transfers between devices, scatter_dp(): return lax.psum_scatter(rows, 'dp', scatter_dimension=0, tiled=True)  103 us
    all_gather x3, waiting for transfers between devices, gather_dp(): return lax.all_gather(rows, 'dp', axis=0, tiled=True)  102 us
    dot_general x12, matrix products, dot(): lax.dot_general(a, b, (contract, ((), ())), preferred_element_type=jnp.fl...  82.6 us
    all_to_all x2, waiting for transfers between devices, exchange_sum(): got = lax.all_to_all(slabs, 'seq', split_axis=0, concat_axis=0, tiled=True)  82.1 us
    unnamed x131, local copies, waits for them, and re-layouts  27.6 us
    convert_element_type x3, local copies, waits for them, and re-layouts, local(): up_full = up_part.reshape(n_seq, own, n_dp, unit).transpose(1, 2, 0, 3).r...  27.3 us
  transfers between devices with their start and end apart: 19, of which 17 were waited for; matrix products, arithmetic and copies ran while one was open for 22% of the time, Pallas kernels for 0%

commit v1 on v0

--- a/solution.py
+++ b/solution.py
@@ -245,7 +245,7 @@
             ],
             axis=1,
         )
-        small = lax.psum(small, ("dp", "seq"))
+        small = jnp.sum(lax.all_gather(small, ("dp", "seq")), axis=0)
         mine = lax.dynamic_index_in_dim(small, lax.axis_index("dp"), 0, keepdims=False)
         g1, s1, g2, s2, bd = (mine[k * own : (k + 1) * own] for k in range(5))
         bq = mine[5 * own : 8 * own]

time: 961 us -> 892 us (0.928)
  waiting for transfers between devices: 690 us -> 622 us
    psum x1 -> x0, waiting for transfers between devices: 107 us -> none  [local(): small = lax.psum(small, ('dp', 'seq'))]
    all_gather x0 -> x1, waiting for transfers between devices: none -> 40.6 us  [local(): small = jnp.sum(lax.all_gather(small, ('dp', 'seq')), axis=0)]
  transfers between devices with their start and end apart: 19 -> 19, of which waited for: 17 -> 17; matrix products, arithmetic and copies ran while one was open for 22% -> 23% of each run, Pallas kernels for 0% -> 0%
where the time goes in v1:
time: 892 us; the launch traced here: 887 us
  waiting for transfers between devices  622 us (70%)
  local copies, waits for them, and re-layouts  99.5 us (11%)
  matrix products  87.6 us (10%)
  other arithmetic  35.9 us (4%)
  starting transfers between devices  19 us (2%)
  between operations  15.1 us (2%)
    all_gather x6, waiting for transfers between devices, gather_seq(): return lax.all_gather(shard, 'seq', axis=0, tiled=False)  239 us
    reduce_scatter x4, waiting for transfers between devices, scatter_dp(): return lax.psum_scatter(rows, 'dp', scatter_dimension=0, tiled=True)  103 us
    all_gather x3, waiting for transfers between devices, gather_dp(): return lax.all_gather(rows, 'dp', axis=0, tiled=True)  102 us
    dot_general x12, matrix products, dot(): lax.dot_general(a, b, (contract, ((), ())), preferred_element_type=jnp.fl...  82.6 us
    all_to_all x2, waiting for transfers between devices, exchange_sum(): got = lax.all_to_all(slabs, 'seq', split_axis=0, concat_axis=0, tiled=True)  82.1 us
    all_gather x1, waiting for transfers between devices, local(): small = jnp.sum(lax.all_gather(small, ('dp', 'seq')), axis=0)  40.6 us
    unnamed x131, local copies, waits for them, and re-layouts  27.6 us
    convert_element_type x3, local copies, waits for them, and re-layouts, local(): up_full = up_part.reshape(n_seq, own, n_dp, unit).transpose(1, 2, 0, 3).r...  27.3 us
  transfers between devices with their start and end apart: 19, of which 17 were waited for; matrix products, arithmetic and copies ran while one was open for 23% of the time, Pallas kernels for 0%

profile of v1, /device:TPU:0, one launch (start us, length us, event | category | flops | bytes accessed | tf_op | source)
XLA Modules:
  0.0 887.2 jit_solution(32343750500598387)
XLA Ops:
  7.9 5.3 all-to-all-start
  13.3 15.4 %all-to-all-done = bf16[8,32,2048]{2,1,0:T(8,128)(2,1)} async-done(((bf16[8,32,2048]{2,1,0:T(8,128)(2,1)}), bf16[8,32,2048]{2,1,0:T(8,128)(2,1)}, u32[]{:S(2)}, u32[]{:S(2)}) %all-to-all-start) | async-done | bytes 1048608 | tf_op jit(solution)/shard_map/all_to_all | solution.py:101
  34.5 6.4 copy.115
  41.0 2.3 constant_dynamic-slice_fusion.2
  43.4 2.3 constant_dynamic-slice_fusion.1
  46.0 8.5 all-gather.7
  61.5 3.4 add_convert_fusion.4
  64.9 21.6 %all-gather.30.cloned.1.call-done = bf16[16,32,2048]{2,1,0:T(8,128)(2,1)} async-done(((bf16[2,32,2048]{2,1,0:T(8,128)(2,1)}), bf16[16,32,2048]{2,1,0:T(8,128)(2,1)}) %all-gather.30.cloned.1.call-update) | async-done | bytes 2097168 | tf_op jit(solution)/shard_map/all_gather | solution.py:106
  88.2 45.5 %all-gather.28.cloned.1.call-done = bf16[4,128,2048]{2,1,0:T(8,128)(2,1)} async-done(((bf16[1,128,2048]{2,1,0:T(8,128)(2,1)}), bf16[4,128,2048]{2,1,0:T(8,128)(2,1)}) %all-gather.28.cloned.1.call-update) | async-done | bytes 2097168 | tf_op jit(solution)/shard_map/all_gather | solution.py:49
  133.7 3.7 convolution_convert_fusion.4
  137.4 42.8 %all-gather.22.cloned.1.call-done = bf16[2048,1536]{1,0:T(8,128)(2,1)} async-done(((bf16[256,1536]{1,0:T(8,128)(2,1)}), bf16[2048,1536]{1,0:T(8,128)(2,1)}) %all-gather.22.cloned.1.call-update) | async-done | bytes 6291472 | tf_op jit(solution)/shard_map/all_gather | solution.py:45
  180.3 8.5 convolution_add_fusion
  188.8 3.9 reshape.392
  205.0 3.8 add_convert_fusion
  218.8 8.2 convolution_convert_fusion.2
  227.1 11.4 %all-gather.24.cloned.1.call-done = bf16[2048,2048]{0,1:T(8,128)(2,1)} async-done(((bf16[256,2048]{0,1:T(8,128)(2,1)}), bf16[2048,2048]{0,1:T(8,128)(2,1)}) %all-gather.24.cloned.1.call-update) | async-done | bytes 8388624 | tf_op jit(solution)/shard_map/all_gather | solution.py:45
  238.5 8.9 %multiply_convert_fusion = (bf16[512,2048]{1,0:T(8,128)(2,1)}, f32[512,2048]{1,0:T(8,128)}) fusion(f32[2048]{0:T(1024)S(1)} %bitcast.208, bf16[512,2048]{1,0:T(8,128)(2,1)S(1)} %copy-done.19, bf16[2048,2048]{0,1:T(8,128)(2,1)} %all-gather.24.cloned.1.call-done), kind=kOutput, calls=%fused_computation.20 | convolution fusion | flops 4301258752 | bytes 16785408 | tf_op jit(solution)/shard_map/dot_general | solution.py:14
  247.4 47.7 %all-gather.26.cloned.1.call-done = bf16[2048,2048]{1,0:T(8,128)(2,1)} async-done(((bf16[256,2048]{1,0:T(8,128)(2,1)}), bf16[2048,2048]{1,0:T(8,128)(2,1)}) %all-gather.26.cloned.1.call-update) | async-done | bytes 8388624 | tf_op jit(solution)/shard_map/all_gather | solution.py:45
  295.1 10.7 %fusion.43 = (f32[2048]{0:T(1024)S(1)}, bf16[512,2048]{1,0:T(8,128)(2,1)S(1)}) fusion(f32[512,2048]{1,0:T(8,128)} %get-tuple-element.106, f32[2048]{0:T(1024)S(1)} %bitcast.209, bf16[2048,2048]{1,0:T(8,128)(2,1)} %all-gather.26.cloned.1.call-done, bf16[512,2048]{1,0:T(8,128)(2,1)} %bitcast.218), kind=kOutput, calls=%fused_computation.143 | convolution fusion | flops 4307548160 | bytes 16793600 | tf_op jit(solution)/shard_map/dot_general | solution.py:14
  307.1 6.8 convolution_convert_fusion.1
  315.5 8.5 convolution_convert_fusion
  325.5 5.8 fusion.45
  331.3 10.5 %fusion.38 = (f32[2048]{0:T(1024)S(1)}, f32[2048]{0:T(1024)S(1)}, bf16[512,2048]{1,0:T(8,128)(2,1)}, f32[2048]{0:T(1024)S(1)}, f32[2048]{0:T(1024)S(1)}) fusion(f32[512]{0:T(512)S(1)} %copy-done.36, f32[512]{0:T(512)S(1)} %copy-done.34, bf16[4,128,2048]{2,1,0:T(8,128)(2,1)S(1)} %copy-done.1, f32[2048]{0:T(1024)S(1)} %bitcast.202, ...), kind=kOutput, calls=%fused_computation.138 | convolution fusion | flops 4308590592 | bytes 18927616 | tf_op jit(solution)/shard_map/dot_general | solution.py:14
  341.8 4.7 all-to-all-start.2
  346.5 7.1 fusion.44
  353.6 2.6 add_convert_fusion.2
  356.2 39.2 %all-to-all-done.2 = bf16[4,128,2048]{2,1,0:T(8,128)(2,1)} async-done(((bf16[4,128,2048]{2,1,0:T(8,128)(2,1)}), bf16[4,128,2048]{2,1,0:T(8,128)(2,1)}, u32[]{:S(2)}, u32[]{:S(2)}) %all-to-all-start.2) | async-done | bytes 2097184 | tf_op jit(solution)/shard_map/all_to_all | solution.py:58
  395.4 4.5 all-to-all-start.1
  402.3 2.3 convert_reduce_fusion
  404.9 43.0 %all-to-all-done.1 = bf16[4,128,2048]{2,1,0:T(8,128)(2,1)} async-done(((bf16[4,128,2048]{2,1,0:T(8,128)(2,1)}), bf16[4,128,2048]{2,1,0:T(8,128)(2,1)}, u32[]{:S(2)}, u32[]{:S(2)}) %all-to-all-start.1) | async-done | bytes 2097184 | tf_op jit(solution)/shard_map/all_to_all | solution.py:58
  453.3 27.5 %reduce-scatter.9.cloned.1.call-done = bf16[256,2048]{1,0:T(8,128)(2,1)} async-done(((bf16[2048,2048]{1,0:T(8,128)(2,1)}), bf16[256,2048]{1,0:T(8,128)(2,1)}) %reduce-scatter.9.cloned.1.call-update) | async-done | bytes 1048592 | tf_op jit(solution)/shard_map/reduce_scatter | solution.py:53
  480.9 75.3 %reduce-scatter.11.cloned.1.call-done = bf16[256,2048]{1,0:T(8,128)(2,1)} async-done(((bf16[2048,2048]{1,0:T(8,128)(2,1)}), bf16[256,2048]{1,0:T(8,128)(2,1)}) %reduce-scatter.11.cloned.1.call-update) | async-done | bytes 1048592 | tf_op jit(solution)/shard_map/reduce_scatter | solution.py:53
  556.3 29.6 %all-gather.36.cloned.1.call-done = bf16[256,2048]{1,0:T(8,128)(2,1)} async-done(((bf16[64,2048]{1,0:T(8,128)(2,1)}), bf16[256,2048]{1,0:T(8,128)(2,1)}) %all-gather.36.cloned.1.call-update) | async-done | bytes 1048592 | tf_op jit(solution)/shard_map/all_gather | solution.py:49
  585.8 3.9 all-to-all-start.3
  589.7 16.0 %all-to-all-done.3 = bf16[8,32,2048]{2,1,0:T(8,128)(2,1)S(1)} async-done(((bf16[8,32,2048]{2,1,0:T(8,128)(2,1)}), bf16[8,32,2048]{2,1,0:T(8,128)(2,1)S(1)}, u32[]{:S(2)}, u32[]{:S(2)}) %all-to-all-start.3) | async-done | bytes 1048608 | tf_op jit(solution)/shard_map/all_to_all | solution.py:215
  607.4 40.6 %all-gather.32.cloned.1.call-done = f32[256,3072]{1,0:T(8,128)} async-done(((f32[8,3072]{1,0:T(8,128)}), f32[256,3072]{1,0:T(8,128)}) %all-gather.32.cloned.1.call-update) | async-done | bytes 3145744 | tf_op jit(solution)/shard_map/all_gather | solution.py:248
  652.1 59.7 %all-gather.34.cloned.1.call-done = bf16[1024,1536]{1,0:T(8,128)(2,1)} async-done(((bf16[256,1536]{1,0:T(8,128)(2,1)}), bf16[1024,1536]{1,0:T(8,128)(2,1)}) %all-gather.34.cloned.1.call-update) | async-done | bytes 3145744 | tf_op jit(solution)/shard_map/all_gather | solution.py:49
  711.8 5.4 copy.128
  717.1 8.2 reshape.417
  725.3 6.6 copy.129
  731.9 6.6 copy.132
  738.5 54.1 %all-gather.38.cloned.1.call-done = bf16[1024,2048]{1,0:T(8,128)(2,1)} async-done(((bf16[256,2048]{1,0:T(8,128)(2,1)}), bf16[1024,2048]{1,0:T(8,128)(2,1)}) %all-gather.38.cloned.1.call-update) | async-done | bytes 4194320 | tf_op jit(solution)/shard_map/all_gather | solution.py:49
  792.6 4.3 copy.158
  796.9 4.1 bitcast_bitcast_fusion
  801.0 12.4 %copy.131 = f32[256,8,4,256]{3,2,1,0:T(4,128)} copy(f32[256,8,4,256]{3,1,0,2:T(8,128)} %bitcast_bitcast_fusion) | data formatting | bytes 16777216 | tf_op jit(solution)/shard_map/convert_element_type | solution.py:205
  813.4 10.7 %reshape.415 = f32[256,8192]{1,0:T(8,128)} reshape(f32[256,8,4,256]{3,2,1,0:T(4,128)} %copy.131) | data formatting | bytes 16777216 | tf_op jit(solution)/shard_map/convert_element_type | solution.py:205
  824.2 49.1 %all-gather.40.cloned.1.call-done = bf16[1024,2048]{1,0:T(8,128)(2,1)} async-done(((bf16[256,2048]{1,0:T(8,128)(2,1)}), bf16[1024,2048]{1,0:T(8,128)(2,1)}) %all-gather.40.cloned.1.call-update) | async-done | bytes 4194320 | tf_op jit(solution)/shard_map/all_gather | solution.py:49
  873.3 6.7 convert_element_type.310
  (232 shorter events, 56.0 us)
Async XLA Ops:
  7.2 24.1 %copy-start.12 = (bf16[256,6144]{1,0:T(8,128)(2,1)S(1)}, bf16[256,6144]{1,0:T(8,128)(2,1)}, u32[]{:S(2)}) copy-start(bf16[256,6144]{1,0:T(8,128)(2,1)} %param.18) | copy-start | bytes 9437188
  7.2 50.8 %all-gather.20.cloned.1.call-start = ((), (), s32[]{:S(2)}) async-start(), calls=%async_computation.8 | async-start | bytes 2621440 | tf_op jit(solution)/shard_map/all_gather | solution.py:49
  7.9 20.8 %all-to-all-start = ((bf16[8,32,2048]{2,1,0:T(8,128)(2,1)}), bf16[8,32,2048]{2,1,0:T(8,128)(2,1)}, u32[]{:S(2)}, u32[]{:S(2)}) async-start(bf16[8,32,2048]{2,1,0:T(8,128)(2,1)} %bitcast.189), calls=%async_computation | async-start | bytes 2097152 | tf_op jit(solution)/shard_map/all_to_all | solution.py:101
  13.3 73.2 %all-gather.30.cloned.1.call-start = ((), (), s32[]{:S(2)}) async-start(), calls=%async_computation.17 | async-start | bytes 2359296 | tf_op jit(solution)/shard_map/all_gather | solution.py:106
  30.4 103.3 %all-gather.28.cloned.1.call-start = ((), (), s32[]{:S(2)}) async-start(), calls=%async_computation.12 | async-start | bytes 2621440 | tf_op jit(solution)/shard_map/all_gather | solution.py:49
  31.2 149.1 %all-gather.22.cloned.1.call-start = ((), (), s32[]{:S(2)}) async-start(), calls=%async_computation.9 | async-start | bytes 7077888 | tf_op jit(solution)/shard_map/all_gather | solution.py:45
  34.5 204.0 %all-gather.24.cloned.1.call-start = ((), (), s32[]{:S(2)}) async-start(), calls=%async_computation.10 | async-start | bytes 9437184 | tf_op jit(solution)/shard_map/all_gather | solution.py:45
  40.9 4.9 copy-start.40
  40.9 4.9 copy-start.41
  40.9 4.9 copy-start.42
  40.9 4.9 copy-start.43
  40.9 4.9 copy-start.44
  40.9 5.0 copy-start.45
  40.9 5.0 copy-start.38
  40.9 5.0 copy-start.39
  43.3 251.8 %all-gather.26.cloned.1.call-start = ((), (), s32[]{:S(2)}) async-start(), calls=%async_computation.11 | async-start | bytes 9437184 | tf_op jit(solution)/shard_map/all_gather | solution.py:45
  45.7 356.4 %reduce-scatter.7.cloned.1.call-start = ((), (), s32[]{:S(2)}) async-start(), calls=%async_computation.14 | async-start | bytes 2359296 | tf_op jit(solution)/shard_map/reduce_scatter | solution.py:53
  58.0 2.2 copy-start
  60.1 4.8 copy-start.33
  61.5 3.4 copy-start.35
  88.2 49.2 %copy-start.6 = (bf16[2,8,32,2048]{3,2,1,0:T(8,128)(2,1)}, bf16[2,8,32,2048]{3,2,1,0:T(8,128)(2,1)S(1)}, u32[]{:S(2)}) copy-start(bf16[2,8,32,2048]{3,2,1,0:T(8,128)(2,1)S(1)} %copy.114) | copy-start | bytes 6291460
  194.6 2.2 copy-start.14
  200.6 1.6 copy-start.46
  205.0 247.6 %reduce-scatter.5.cloned.1.call-start = ((), (), s32[]{:S(2)}) async-start(), calls=%async_computation.13 | async-start | bytes 7077888 | tf_op jit(solution)/shard_map/reduce_scatter | solution.py:53
  205.0 3.8 copy-start.32
  227.0 11.5 %copy-start.19 = (bf16[512,2048]{1,0:T(8,128)(2,1)S(1)}, bf16[512,2048]{1,0:T(8,128)(2,1)}, u32[]{:S(2)}) copy-start(bf16[512,2048]{1,0:T(8,128)(2,1)} %get-tuple-element.68) | copy-start | bytes 6291460
  227.0 253.8 %reduce-scatter.9.cloned.1.call-start = ((), (), s32[]{:S(2)}) async-start(), calls=%async_computation.15 | async-start | bytes 9437184 | tf_op jit(solution)/shard_map/reduce_scatter | solution.py:53
  313.9 1.6 copy-start.47
  313.9 242.3 %reduce-scatter.11.cloned.1.call-start = ((), (), s32[]{:S(2)}) async-start(), calls=%async_computation.16 | async-start | bytes 9437184 | tf_op jit(solution)/shard_map/reduce_scatter | solution.py:53
  325.4 5.8 copy-start.1
  325.4 5.8 copy-start.34
  325.4 5.8 copy-start.36
  325.4 5.8 copy-start.50
  341.8 4.7 copy-start.48
  341.8 53.6 %all-to-all-start.2 = ((bf16[4,128,2048]{2,1,0:T(8,128)(2,1)}), bf16[4,128,2048]{2,1,0:T(8,128)(2,1)}, u32[]{:S(2)}, u32[]{:S(2)}) async-start(bf16[4,128,2048]{2,1,0:T(8,128)(2,1)} %bitcast.31), calls=%async_computation.2 | async-start | bytes 4194304 | tf_op jit(solution)/shard_map/all_to_all | solution.py:58
  346.5 7.1 copy-start.7
  346.5 7.1 copy-start.11
  356.2 43.8 %copy-start.2 = (bf16[1,128,2048]{2,1,0:T(8,128)(2,1)S(1)}, bf16[1,128,2048]{2,1,0:T(8,128)(2,1)}, u32[]{:S(2)}) copy-start(bf16[1,128,2048]{2,1,0:T(8,128)(2,1)} %param.14) | copy-start | bytes 1572868
  356.2 44.3 %copy-start.4 = (f32[512,1,2,256]{3,0,2,1:T(8,128)S(1)}, f32[512,1,2,256]{3,0,2,1:T(8,128)}, u32[]{:S(2)}) copy-start(f32[512,1,2,256]{3,0,2,1:T(8,128)} %copy-done.3) | copy-start | bytes 3145732
  395.4 52.4 %all-to-all-start.1 = ((bf16[4,128,2048]{2,1,0:T(8,128)(2,1)}), bf16[4,128,2048]{2,1,0:T(8,128)(2,1)}, u32[]{:S(2)}, u32[]{:S(2)}) async-start(bf16[4,128,2048]{2,1,0:T(8,128)(2,1)} %bitcast.15), calls=%async_computation.1 | async-start | bytes 4194304 | tf_op jit(solution)/shard_map/all_to_all | solution.py:58
  399.9 186.0 %all-gather.36.cloned.1.call-start = ((), (), s32[]{:S(2)}) async-start(), calls=%async_computation.20 | async-start | bytes 1310720 | tf_op jit(solution)/shard_map/all_gather | solution.py:49
  402.1 245.9 %all-gather.32.cloned.1.call-start = ((), (), s32[]{:S(2)}) async-start(), calls=%async_computation.18 | async-start | bytes 3244032 | tf_op jit(solution)/shard_map/all_gather | solution.py:248
  404.5 45.4 %copy-start.13 = (bf16[1,128,2048]{2,1,0:T(8,128)(2,1)S(1)}, bf16[1,128,2048]{2,1,0:T(8,128)(2,1)}, u32[]{:S(2)}) copy-start(bf16[1,128,2048]{2,1,0:T(8,128)(2,1)} %param.15) | copy-start | bytes 1572868
  452.5 259.2 %all-gather.34.cloned.1.call-start = ((), (), s32[]{:S(2)}) async-start(), calls=%async_computation.19 | async-start | bytes 3932160 | tf_op jit(solution)/shard_map/all_gather | solution.py:49
  453.3 339.3 %all-gather.38.cloned.1.call-start = ((), (), s32[]{:S(2)}) async-start(), calls=%async_computation.21 | async-start | bytes 5242880 | tf_op jit(solution)/shard_map/all_gather | solution.py:49
  480.9 392.4 %all-gather.40.cloned.1.call-start = ((), (), s32[]{:S(2)}) async-start(), calls=%async_computation.22 | async-start | bytes 5242880 | tf_op jit(solution)/shard_map/all_gather | solution.py:49
  585.8 19.9 %all-to-all-start.3 = ((bf16[8,32,2048]{2,1,0:T(8,128)(2,1)}), bf16[8,32,2048]{2,1,0:T(8,128)(2,1)S(1)}, u32[]{:S(2)}, u32[]{:S(2)}) async-start(bf16[8,32,2048]{2,1,0:T(8,128)(2,1)} %bitcast.190), calls=%async_computation.5 | async-start | bytes 2097152 | tf_op jit(solution)/shard_map/all_to_all | solution.py:215
  651.4 228.6 %copy-start.37 = (f32[1,256]{1,0:T(1,128)}, f32[1,256]{1,0:T(1,128)S(1)}, u32[]{:S(2)}) copy-start(f32[1,256]{1,0:T(1,128)S(1)} %get-tuple-element.91) | copy-start | bytes 3076
  (22 other events, 29.1 us)
Sparse Core Ops, SparseCore 0:
  9.6 48.3 all-gather.19
  59.9 26.5 all-gather.29
  88.1 45.6 all-gather.27
  136.1 44.1 all-gather.21
  182.6 55.8 all-gather.23
  240.8 54.2 all-gather.25
  298.4 41.1 reduce-scatter.6
  343.5 61.7 reduce-scatter.4
  409.3 71.4 reduce-scatter.8
  484.7 71.4 reduce-scatter.10
  557.8 27.9 all-gather.35
  588.6 59.3 all-gather.31
  649.6 62.1 all-gather.33
  713.2 79.3 all-gather.37
  794.0 79.2 all-gather.39
